TPU v7x, 32 devices: a whole 2x2x4 slice. The times are simulated.
32 devices in a mesh: fsdp: 4 (over y, x), ep: 8 (over z, core).
Axes of the slice: x: 2, y: 2, z: 4, core: 2. Of those that a mesh axis runs over, the one named last changes fastest.
Arguments:
- hidden_in: bfloat16 [8192, 2048], P(('fsdp', 'ep')), may hold values from -6 to 6
- norm_gain: float32 [2048], replicated, may hold values from 0.25 to 1.75
- expert_ids: int32 [8192, 8], P(('fsdp', 'ep')), may hold values from 0 to 15, all different within a row; in each aligned block of 256 rows (0 to 255, 256 to 511, ...) at most 160 rows name the same one
- expert_probs: float32 [8192, 8], P(('fsdp', 'ep')), may hold values from 0.05 to 0.25
- gate_proj: bfloat16 [16, 2048, 768], P('ep', 'fsdp'), may hold values from -0.125 to 0.125
- up_proj: bfloat16 [16, 2048, 768], P('ep', 'fsdp'), may hold values from -0.125 to 0.125
- down_proj: bfloat16 [16, 768, 2048], P('ep', None, 'fsdp'), may hold values from -0.21875 to 0.21875
Outputs:
- moe_out: bfloat16 [8192, 2048], P(('fsdp', 'ep'))
Inputs may be any that keep to these rules, and one draw needn't show every extreme that they name: `expert_ids`: within the rows of one device (aligned blocks of 256 rows) each expert id is named by at most 160 rows, and in some blocks one expert by exactly 160; the 8 ids of a row are distinct.
All inputs are finite; a program needn't handle non-finite values.
Results may differ from a plain program's by a relative error of at most 0.0025.
Values may be sent and summed in bfloat16 or wider, within the bound.
A program may use at most 128 MiB of HBM per device.

v0:
```python
import jax
import jax.numpy as jnp
from jax import lax
from jax.sharding import PartitionSpec as P


def rms_norm(hidden_in, norm_gain):
    values = hidden_in.astype(jnp.float32)
    spread = jnp.mean(values * values, axis=-1, keepdims=True)
    return (values * lax.rsqrt(spread + 1e-06) * norm_gain).astype(jnp.bfloat16)


def per_device(hidden_in, norm_gain, expert_ids, expert_probs, gate_proj, up_proj, down_proj):
    local_experts = gate_proj.shape[0]
    normed = rms_norm(hidden_in, norm_gain)
    all_experts = local_experts * lax.axis_size("ep")
    hot = expert_ids[:, :, None] == jnp.arange(all_experts, dtype=jnp.int32)
    weights = jnp.sum(jnp.where(hot, expert_probs[:, :, None], 0.0), axis=1)
    tokens = lax.all_gather(normed, "ep", axis=0, tiled=True)
    routed = lax.all_to_all(
        weights.reshape(weights.shape[0], lax.axis_size("ep"), local_experts),
        "ep",
        split_axis=1,
        concat_axis=0,
        tiled=True,
    ).reshape(tokens.shape[0], local_experts)
    total = 0.0
    gate_all = lax.all_gather(gate_proj, "fsdp", axis=1, tiled=True)
    up_all = lax.all_gather(up_proj, "fsdp", axis=1, tiled=True)
    down_all = lax.all_gather(down_proj, "fsdp", axis=2, tiled=True)
    for e in range(local_experts):
        gate = jnp.dot(tokens, gate_all[e], preferred_element_type=jnp.float32)
        up = jnp.dot(tokens, up_all[e], preferred_element_type=jnp.float32)
        act = (jax.nn.silu(gate) * up).astype(jnp.bfloat16)
        out = jnp.dot(act, down_all[e], preferred_element_type=jnp.float32).astype(jnp.bfloat16)
        total = total + out.astype(jnp.float32) * routed[:, e, None]
    combined = lax.psum_scatter(total, "ep", scatter_dimension=0, tiled=True)
    return combined.astype(jnp.bfloat16)


def solution(mesh):
    return jax.shard_map(
        per_device,
        mesh=mesh,
        in_specs=(
            P(("fsdp", "ep"), None),
            P(),
            P(("fsdp", "ep"), None),
            P(("fsdp", "ep"), None),
            P("ep", "fsdp", None),
            P("ep", "fsdp", None),
            P("ep", None, "fsdp"),
        ),
        out_specs=P(("fsdp", "ep"), None),
        check_vma=False,
    )
```

profile of v0, /device:TPU:0, one launch (start us, length us, event | category | flops | bytes accessed | tf_op | source)
XLA Modules:
  0.0 533.1 jit_solution(4729882364466384271)
XLA Ops:
  6.5 0.0 all-gather.7.cloned.1.call-start
  6.5 0.7 all-gather.7.cloned.1.call-update
  7.3 0.0 all-gather.5.cloned.1.call-start
  7.3 1.5 fusion.5
  8.8 2.5 fusion.7
  11.3 0.0 all-gather.5.cloned.1.call-update
  11.4 0.0 all-gather.9.cloned.1.call-start
  11.4 0.7 all-gather.9.cloned.1.call-update
  12.1 0.0 all-gather.11.cloned.1.call-start
  12.1 0.5 all-gather.11.cloned.1.call-update
  12.7 0.0 reduce-scatter.2.cloned.1.call-start
  12.7 0.0 copy-done
  12.8 11.8 %all_to_all.15 = f32[256,8,2]{0,2,1:T(2,128)S(1)} all-to-all(f32[256,8,2]{0,2,1:T(2,128)S(1)} %reshape.18), channel_id=1, replica_groups=mesh['fsdp'=4,'ep'=8] {'ep'}, dimensions={1} | all-to-all | bytes 32768 | tf_op jit(solution)/shard_map/all_to_all | solution.py:20
  24.6 57.4 %all-gather.7.cloned.1.call-done = bf16[2,2048,768]{2,1,0:T(8,128)(2,1)} async-done(((bf16[2,512,768]{2,1,0:T(8,128)(2,1)}), bf16[2,2048,768]{2,1,0:T(8,128)(2,1)}) %all-gather.7.cloned.1.call-update) | async-done | bytes 6291472 | tf_op jit(solution)/shard_map/all_gather | solution.py:28
  82.0 83.7 %all-gather.5.cloned.1.call-done = bf16[2048,2048]{1,0:T(8,128)(2,1)} async-done(((bf16[256,2048]{1,0:T(8,128)(2,1)}), bf16[2048,2048]{1,0:T(8,128)(2,1)}) %all-gather.5.cloned.1.call-update) | async-done | bytes 8388624 | tf_op jit(solution)/shard_map/all_gather | solution.py:19
  165.6 11.8 %fusion.1 = f32[2048,768]{1,0:T(8,128)} fusion(bf16[2048,2048]{1,0:T(8,128)(2,1)} %all-gather.5.cloned.1.call-done, bf16[2,2048,768]{2,1,0:T(8,128)(2,1)} %all-gather.7.cloned.1.call-done), kind=kOutput, calls=%fused_computation.7 | convolution fusion | flops 6442450944 | bytes 17825792 | tf_op jit(solution)/shard_map/dot_general | solution.py:32
  177.4 8.5 %fusion.2 = f32[2048,768]{1,0:T(8,128)} fusion(bf16[2048,2048]{1,0:T(8,128)(2,1)S(1)} %copy-done.2, bf16[2,2048,768]{2,1,0:T(8,128)(2,1)S(1)} %copy-done.3), kind=kOutput, calls=%fused_computation.11 | convolution fusion | flops 6442450944 | bytes 17825792 | tf_op jit(solution)/shard_map/dot_general | solution.py:32
  185.9 50.1 %all-gather.9.cloned.1.call-done = bf16[2,2048,768]{2,1,0:T(8,128)(2,1)} async-done(((bf16[2,512,768]{2,1,0:T(8,128)(2,1)}), bf16[2,2048,768]{2,1,0:T(8,128)(2,1)}) %all-gather.9.cloned.1.call-update) | async-done | bytes 6291472 | tf_op jit(solution)/shard_map/all_gather | solution.py:29
  236.0 71.6 %all-gather.11.cloned.1.call-done = bf16[2,768,2048]{2,1,0:T(8,128)(2,1)} async-done(((bf16[2,768,512]{2,1,0:T(8,128)(2,1)}), bf16[2,768,2048]{2,1,0:T(8,128)(2,1)}) %all-gather.11.cloned.1.call-update) | async-done | bytes 6291472 | tf_op jit(solution)/shard_map/all_gather | solution.py:30
  307.6 22.1 %fusion = bf16[2048,2048]{1,0:T(8,128)(2,1)} fusion(f32[2048,768]{1,0:T(8,128)} %fusion.2, bf16[2048,2048]{1,0:T(8,128)(2,1)} %all-gather.5.cloned.1.call-done, bf16[2,768,2048]{2,1,0:T(8,128)(2,1)} %all-gather.11.cloned.1.call-done, bf16[2,2048,768]{2,1,0:T(8,128)(2,1)} %all-gather.9.cloned.1.call-done), kind=kOutput, calls=%fused_computation.3 | convolution fusion | flops 12894339072 | bytes 29360128 | tf_op jit(solution)/shard_map/dot_general | solution.py:35
  329.7 25.8 %multiply_add_fusion = f32[2048,2048]{1,0:T(8,128)} fusion(f32[2048]{0:T(1024)S(1)} %bitcast.35, f32[2048]{0:T(1024)S(1)} %bitcast.34, bf16[2048,2048]{1,0:T(8,128)(2,1)} %fusion, f32[2048,768]{1,0:T(8,128)} %fusion.1, bf16[2048,2048]{1,0:T(8,128)(2,1)} %all-gather.5.cloned.1.call-done, bf16[2,768,2048]{2,1,0:T(8,128)(2,1)} %all-gather.11.cloned.1.call-done, ...), kind=kOutput, calls=%fused_computation | convolution fusion | flops 12919504896 | bytes 46153728 | tf_op jit(solution)/shard_map/dot_general | solution.py:35
  355.5 0.0 reduce-scatter.2.cloned.1.call-update
  355.5 168.3 %reduce-scatter.2.cloned.1.call-done = f32[256,2048]{1,0:T(8,128)} async-done(((f32[2048,2048]{1,0:T(8,128)}), f32[256,2048]{1,0:T(8,128)}) %reduce-scatter.2.cloned.1.call-update) | async-done | bytes 2097168 | tf_op jit(solution)/shard_map/reduce_scatter | solution.py:37
  523.8 2.7 convert_element_type.35
  (11 shorter events, 0.1 us)
Async XLA Ops:
  6.5 6.2 %copy-start = (f32[256,8]{0,1:T(8,128)S(1)}, f32[256,8]{0,1:T(8,128)}, u32[]{:S(2)}) copy-start(f32[256,8]{0,1:T(8,128)} %param.10) | copy-start | bytes 24580
  6.5 6.2 %copy-start.1 = (s32[256,8]{0,1:T(8,128)S(1)}, s32[256,8]{0,1:T(8,128)}, u32[]{:S(2)}) copy-start(s32[256,8]{0,1:T(8,128)} %param.9) | copy-start | bytes 24580
  6.5 75.4 %all-gather.7.cloned.1.call-start = ((), (), s32[]{:S(2)}) async-start(), calls=%async_computation.3 | async-start | bytes 7864320 | tf_op jit(solution)/shard_map/all_gather | solution.py:28
  7.3 158.4 %all-gather.5.cloned.1.call-start = ((), (), s32[]{:S(2)}) async-start(), calls=%async_computation.2 | async-start | bytes 9437184 | tf_op jit(solution)/shard_map/all_gather | solution.py:19
  11.4 224.7 %all-gather.9.cloned.1.call-start = ((), (), s32[]{:S(2)}) async-start(), calls=%async_computation.4 | async-start | bytes 7864320 | tf_op jit(solution)/shard_map/all_gather | solution.py:29
  12.1 295.5 %all-gather.11.cloned.1.call-start = ((), (), s32[]{:S(2)}) async-start(), calls=%async_computation.5 | async-start | bytes 7864320 | tf_op jit(solution)/shard_map/all_gather | solution.py:30
  12.7 511.2 %reduce-scatter.2.cloned.1.call-start = ((), (), s32[]{:S(2)}) async-start(), calls=%async_computation.6 | async-start | bytes 18874368 | tf_op jit(solution)/shard_map/reduce_scatter | solution.py:37
  165.6 11.8 %copy-start.2 = (bf16[2048,2048]{1,0:T(8,128)(2,1)S(1)}, bf16[2048,2048]{1,0:T(8,128)(2,1)}, u32[]{:S(2)}) copy-start(bf16[2048,2048]{1,0:T(8,128)(2,1)} %all-gather.5.cloned.1.call-done) | copy-start | bytes 25165828
  165.6 11.8 %copy-start.3 = (bf16[2,2048,768]{2,1,0:T(8,128)(2,1)S(1)}, bf16[2,2048,768]{2,1,0:T(8,128)(2,1)}, u32[]{:S(2)}) copy-start(bf16[2,2048,768]{2,1,0:T(8,128)(2,1)} %all-gather.7.cloned.1.call-done) | copy-start | bytes 18874372
Sparse Core Ops, SparseCore 0:
  9.2 72.7 all-gather.6
  83.6 82.0 all-gather.4
  167.5 68.5 all-gather.8
  237.7 69.8 all-gather.10
  355.6 168.1 reduce-scatter.1
where the time goes:
time: 533 us
  waiting for transfers between devices  433 us (81%)
  matrix products  68.2 us (13%)
  between operations  13.2 us (2%)
  blocking collectives  11.8 us (2%)
  other arithmetic  6.76 us (1%)
    reduce_scatter x1, waiting for transfers between devices, per_device(): combined = lax.psum_scatter(total, 'ep', scatter_dimension=0, tiled=True)  168 us
    all_gather x1, waiting for transfers between devices, per_device(): tokens = lax.all_gather(normed, 'ep', axis=0, tiled=True)  83.7 us
    all_gather x1, waiting for transfers between devices, per_device(): down_all = lax.all_gather(down_proj, 'fsdp', axis=2, tiled=True)  71.6 us
    all_gather x1, waiting for transfers between devices, per_device(): gate_all = lax.all_gather(gate_proj, 'fsdp', axis=1, tiled=True)  57.4 us
    all_gather x1, waiting for transfers between devices, per_device(): up_all = lax.all_gather(up_proj, 'fsdp', axis=1, tiled=True)  50.1 us
    dot_general x2, matrix products, per_device(): jnp.dot(act, down_all[e], preferred_element_type=jnp.float32)  47.9 us
    dot_general x2, matrix products, per_device(): gate = jnp.dot(tokens, gate_all[e], preferred_element_type=jnp.float32)  20.3 us
    all_to_all x1, blocking collectives, per_device(): lax.all_to_all(weights.reshape(weights.shape[0], lax.axis_size('ep'), loc...  11.8 us
  transfers between devices with their start and end apart: 5, of which 5 were waited for; matrix products, arithmetic and copies ran while one was open for 5% of the time, Pallas kernels for 0%

commit v1 on v0

--- a/solution.py
+++ b/solution.py
@@ -26,7 +26,8 @@
     ).reshape(tokens.shape[0], local_experts)
     total = 0.0
     gate_all = lax.all_gather(gate_proj, "fsdp", axis=1, tiled=True)
-    up_all = lax.all_gather(up_proj, "fsdp", axis=1, tiled=True)
+    r2 = jax.lax.all_gather(up_proj, "fsdp")
+    up_all = jnp.concatenate(r2, axis=1)
     down_all = lax.all_gather(down_proj, "fsdp", axis=2, tiled=True)
     for e in range(local_experts):
         gate = jnp.dot(tokens, gate_all[e], preferred_element_type=jnp.float32)

time: 533 us -> 532 us (level)
    all_gather x1, waiting for transfers between devices: 71.6 us -> 49.8 us  [per_device(): down_all = lax.all_gather(down_proj, 'fsdp', axis=2, tiled=True)]
    all_gather x1, waiting for transfers between devices: 57.4 us -> 66.9 us  [per_device(): gate_all = lax.all_gather(gate_proj, 'fsdp', axis=1, tiled=True)]
    all_gather x1, waiting for transfers between devices: 50.1 us -> 57.3 us  [per_device(): r2 = jax.lax.all_gather(up_proj, 'fsdp')]
  transfers between devices with their start and end apart: 5 -> 5, of which waited for: 5 -> 5; matrix products, arithmetic and copies ran while one was open for 5% -> 6% of each run, Pallas kernels for 0% -> 0%
where the time goes in v1:
time: 532 us
  waiting for transfers between devices  428 us (80%)
  matrix products  67.1 us (13%)
  between operations  13.2 us (2%)
  blocking collectives  11.8 us (2%)
  other arithmetic  6.76 us (1%)
    reduce_scatter x1, waiting for transfers between devices, per_device(): combined = lax.psum_scatter(total, 'ep', scatter_dimension=0, tiled=True)  168 us
    all_gather x1, waiting for transfers between devices, per_device(): tokens = lax.all_gather(normed, 'ep', axis=0, tiled=True)  83.7 us
    all_gather x1, waiting for transfers between devices, per_device(): gate_all = lax.all_gather(gate_proj, 'fsdp', axis=1, tiled=True)  66.9 us
    all_gather x1, waiting for transfers between devices, per_device(): r2 = jax.lax.all_gather(up_proj, 'fsdp')  57.3 us
    all_gather x1, waiting for transfers between devices, per_device(): down_all = lax.all_gather(down_proj, 'fsdp', axis=2, tiled=True)  49.8 us
    dot_general x2, matrix products, per_device(): jnp.dot(act, down_all[e], preferred_element_type=jnp.float32)  46.8 us
    dot_general x2, matrix products, per_device(): gate = jnp.dot(tokens, gate_all[e], preferred_element_type=jnp.float32)  20.3 us
    all_to_all x1, blocking collectives, per_device(): lax.all_to_all(weights.reshape(weights.shape[0], lax.axis_size('ep'), loc...  11.8 us
  transfers between devices with their start and end apart: 5, of which 5 were waited for; matrix products, arithmetic and copies ran while one was open for 6% of the time, Pallas kernels for 0%

profile of v1, /device:TPU:0, one launch (start us, length us, event | category | flops | bytes accessed | tf_op | source)
XLA Modules:
  0.0 532.0 jit_solution(10498136149874995461)
XLA Ops:
  6.5 0.0 all-gather.12.cloned.1.call-start
  6.5 0.7 all-gather.12.cloned.1.call-update
  7.3 0.0 all-gather.8.cloned.1.call-start
  7.3 0.7 all-gather.8.cloned.1.call-update
  8.0 0.0 all-gather.6.cloned.1.call-start
  8.1 1.5 fusion.5
  9.6 2.5 fusion.7
  12.1 0.0 all-gather.6.cloned.1.call-update
  12.1 0.0 all-gather.10.cloned.1.call-start
  12.2 0.5 all-gather.10.cloned.1.call-update
  12.7 0.0 reduce-scatter.2.cloned.1.call-start
  12.8 11.8 %all_to_all.15 = f32[256,8,2]{0,2,1:T(2,128)S(1)} all-to-all(f32[256,8,2]{0,2,1:T(2,128)S(1)} %reshape.27), channel_id=1, replica_groups=mesh['fsdp'=4,'ep'=8] {'ep'}, dimensions={1} | all-to-all | bytes 32768 | tf_op jit(solution)/shard_map/all_to_all | solution.py:20
  24.6 57.3 %all-gather.12.cloned.1.call-done = bf16[8,512,768]{2,1,0:T(8,128)(2,1)} async-done(((bf16[2,512,768]{2,1,0:T(8,128)(2,1)}), bf16[8,512,768]{2,1,0:T(8,128)(2,1)}) %all-gather.12.cloned.1.call-update) | async-done | bytes 6291472 | tf_op jit(solution)/shard_map/all_gather | solution.py:29
  82.0 5.0 fusion.10
  86.9 66.9 %all-gather.8.cloned.1.call-done = bf16[2,2048,768]{2,1,0:T(8,128)(2,1)} async-done(((bf16[2,512,768]{2,1,0:T(8,128)(2,1)}), bf16[2,2048,768]{2,1,0:T(8,128)(2,1)}) %all-gather.8.cloned.1.call-update) | async-done | bytes 6291472 | tf_op jit(solution)/shard_map/all_gather | solution.py:28
  153.9 83.7 %all-gather.6.cloned.1.call-done = bf16[2048,2048]{1,0:T(8,128)(2,1)} async-done(((bf16[256,2048]{1,0:T(8,128)(2,1)}), bf16[2048,2048]{1,0:T(8,128)(2,1)}) %all-gather.6.cloned.1.call-update) | async-done | bytes 8388624 | tf_op jit(solution)/shard_map/all_gather | solution.py:19
  237.5 11.8 %fusion.1 = f32[2048,768]{1,0:T(8,128)} fusion(bf16[2048,2048]{1,0:T(8,128)(2,1)} %all-gather.6.cloned.1.call-done, bf16[2,2048,768]{2,1,0:T(8,128)(2,1)} %all-gather.8.cloned.1.call-done), kind=kOutput, calls=%fused_computation.6 | convolution fusion | flops 6442450944 | bytes 17825792 | tf_op jit(solution)/shard_map/dot_general | solution.py:33
  249.3 8.5 %fusion.2 = f32[2048,768]{1,0:T(8,128)} fusion(bf16[2048,2048]{1,0:T(8,128)(2,1)S(1)} %copy-done.2, bf16[2,2048,768]{2,1,0:T(8,128)(2,1)S(1)} %copy-done.3), kind=kOutput, calls=%fused_computation.9 | convolution fusion | flops 6442450944 | bytes 17825792 | tf_op jit(solution)/shard_map/dot_general | solution.py:33
  257.8 49.8 %all-gather.10.cloned.1.call-done = bf16[2,768,2048]{2,1,0:T(8,128)(2,1)} async-done(((bf16[2,768,512]{2,1,0:T(8,128)(2,1)}), bf16[2,768,2048]{2,1,0:T(8,128)(2,1)}) %all-gather.10.cloned.1.call-update) | async-done | bytes 6291472 | tf_op jit(solution)/shard_map/all_gather | solution.py:31
  307.6 22.1 %fusion = bf16[2048,2048]{1,0:T(8,128)(2,1)} fusion(f32[2048,768]{1,0:T(8,128)} %fusion.2, bf16[2048,2048]{1,0:T(8,128)(2,1)} %all-gather.6.cloned.1.call-done, bf16[2048,768]{1,0:T(8,128)(2,1)} %bitcast.34, bf16[2,768,2048]{2,1,0:T(8,128)(2,1)} %all-gather.10.cloned.1.call-done), kind=kOutput, calls=%fused_computation.3 | convolution fusion | flops 12894339072 | bytes 29360128 | tf_op jit(solution)/shard_map/dot_general | solution.py:36
  329.7 24.7 %multiply_add_fusion = f32[2048,2048]{1,0:T(8,128)} fusion(f32[2048]{0:T(1024)S(1)} %bitcast.37, f32[2048]{0:T(1024)S(1)} %bitcast.36, bf16[2048,2048]{1,0:T(8,128)(2,1)} %fusion, f32[2048,768]{1,0:T(8,128)} %fusion.1, bf16[2048,2048]{1,0:T(8,128)(2,1)} %all-gather.6.cloned.1.call-done, bf16[2048,768]{1,0:T(8,128)(2,1)S(1)} %bitcast.33, ...), kind=kOutput, calls=%fused_computation | convolution fusion | flops 12919504896 | bytes 46153728 | tf_op jit(solution)/shard_map/dot_general | solution.py:36
  354.4 0.0 reduce-scatter.2.cloned.1.call-update
  354.5 168.3 %reduce-scatter.2.cloned.1.call-done = f32[256,2048]{1,0:T(8,128)} async-done(((f32[2048,2048]{1,0:T(8,128)}), f32[256,2048]{1,0:T(8,128)}) %reduce-scatter.2.cloned.1.call-update) | async-done | bytes 2097168 | tf_op jit(solution)/shard_map/reduce_scatter | solution.py:38
  522.8 2.7 convert_element_type.35
  (12 shorter events, 0.1 us)
Async XLA Ops:
  6.5 6.2 %copy-start = (f32[256,8]{0,1:T(8,128)S(1)}, f32[256,8]{0,1:T(8,128)}, u32[]{:S(2)}) copy-start(f32[256,8]{0,1:T(8,128)} %param.10) | copy-start | bytes 24580
  6.5 6.2 %copy-start.1 = (s32[256,8]{0,1:T(8,128)S(1)}, s32[256,8]{0,1:T(8,128)}, u32[]{:S(2)}) copy-start(s32[256,8]{0,1:T(8,128)} %param.9) | copy-start | bytes 24580
  6.5 75.4 %all-gather.12.cloned.1.call-start = ((), (), s32[]{:S(2)}) async-start(), calls=%async_computation.6 | async-start | bytes 7864320 | tf_op jit(solution)/shard_map/all_gather | solution.py:29
  7.3 146.6 %all-gather.8.cloned.1.call-start = ((), (), s32[]{:S(2)}) async-start(), calls=%async_computation.3 | async-start | bytes 7864320 | tf_op jit(solution)/shard_map/all_gather | solution.py:28
  8.0 229.5 %all-gather.6.cloned.1.call-start = ((), (), s32[]{:S(2)}) async-start(), calls=%async_computation.2 | async-start | bytes 9437184 | tf_op jit(solution)/shard_map/all_gather | solution.py:19
  12.1 295.5 %all-gather.10.cloned.1.call-start = ((), (), s32[]{:S(2)}) async-start(), calls=%async_computation.4 | async-start | bytes 7864320 | tf_op jit(solution)/shard_map/all_gather | solution.py:31
  12.7 510.1 %reduce-scatter.2.cloned.1.call-start = ((), (), s32[]{:S(2)}) async-start(), calls=%async_computation.5 | async-start | bytes 18874368 | tf_op jit(solution)/shard_map/reduce_scatter | solution.py:38
  237.5 11.8 %copy-start.2 = (bf16[2048,2048]{1,0:T(8,128)(2,1)S(1)}, bf16[2048,2048]{1,0:T(8,128)(2,1)}, u32[]{:S(2)}) copy-start(bf16[2048,2048]{1,0:T(8,128)(2,1)} %all-gather.6.cloned.1.call-done) | copy-start | bytes 25165828
  237.5 11.8 %copy-start.3 = (bf16[2,2048,768]{2,1,0:T(8,128)(2,1)S(1)}, bf16[2,2048,768]{2,1,0:T(8,128)(2,1)}, u32[]{:S(2)}) copy-start(bf16[2,2048,768]{2,1,0:T(8,128)(2,1)} %all-gather.8.cloned.1.call-done) | copy-start | bytes 18874372
Sparse Core Ops, SparseCore 0:
  9.2 72.7 all-gather.11
  83.8 70.0 all-gather.7
  155.5 82.0 all-gather.5
  239.2 68.3 all-gather.9
  354.6 168.1 reduce-scatter.1
